TPU v7x, 32 devices: a whole 2x2x4 slice. The times are simulated.
32 devices in a mesh: rep: 4 (over z), exp: 4 (over x, core), shard: 2 (over y).
Axes of the slice: x: 2, y: 2, z: 4, core: 2. Of those that a mesh axis runs over, the one named last changes fastest.
Arguments:
- tokens: bfloat16 [3584, 2048], P(('rep', 'exp', 'shard')), may hold values from -1.5 to 1.5
- routes: int32 [3584, 2], P(('rep', 'exp', 'shard')), may hold values from 0 to 3, all different within a row; in each aligned block of 112 rows (0 to 111, 112 to 223, ...) at most 63 rows name the same one
- gate_weight: bfloat16 [4, 2048, 7168], P('exp', None, 'shard'), may hold values from -0.125 to 0.125
- gate_cotangent: bfloat16 [4, 2016, 7168], P('exp', 'rep', 'shard'), may hold values from -0.75 to 0.75
Outputs:
- token_grad: bfloat16 [3584, 2048], P(('rep', 'exp', 'shard'))
- weight_grad: bfloat16 [4, 2048, 7168], P('exp', None, 'shard')
Inputs may be any that keep to these rules, and one draw needn't show every extreme that they name: `routes`: the two entries of a row differ. The rows of one device name one expert at most 63 times, and some device names some expert exactly 63 times.
All inputs are finite; a program needn't handle non-finite values.
Results may differ from a plain program's by a relative error of at most 0.015.
Values may be sent and summed in bfloat16 or wider, within the bound.
No kernel may reach another device: no remote copies, remote signals or barrier semaphores. Data moves between devices by JAX's collectives and lax.ppermute only.
A program may use at most 128 MiB of HBM per device.

v0:
```python
import jax
import jax.numpy as jnp
from jax import lax
from jax.sharding import PartitionSpec as P


def slot_matrix(route_rows, experts, slot_cap):
    expert_ids = jnp.arange(experts, dtype=jnp.int32)
    onehot = (route_rows[:, :, None] == expert_ids[None, None, :]).astype(jnp.int32)
    flattened = onehot.reshape(-1, experts)
    before = jnp.cumsum(flattened, axis=0) - flattened
    position = jnp.sum(before * flattened, axis=1)
    target = jnp.sum(flattened * expert_ids[None, :], axis=1) * slot_cap + position
    slot_ids = jnp.arange(experts * slot_cap, dtype=jnp.int32)
    matches = (target[None, :] == slot_ids[:, None]).astype(jnp.int32)
    return matches.reshape(experts * slot_cap, -1, 2).sum(axis=2)


def body(tokens, routes, gate_weight, gate_cotangent):
    experts = lax.axis_size("exp")
    shards = lax.axis_size("shard")
    features = tokens.shape[1]
    cotangent = gate_cotangent[0]
    hidden = cotangent.shape[1]
    slot_cap = cotangent.shape[0] // (experts * shards)
    weight = gate_weight[0]
    blocks = cotangent.reshape(experts, shards, slot_cap, hidden)
    placing = slot_matrix(routes, experts, slot_cap).astype(jnp.bfloat16)
    outgoing = jnp.dot(placing, tokens, preferred_element_type=jnp.float32).astype(jnp.bfloat16)
    outgoing = outgoing.reshape(experts, slot_cap, features)
    contract_rows = (((0,), (0,)), ((), ()))
    copies = jnp.broadcast_to(outgoing[:, None], (experts, shards, slot_cap, features))
    copies = copies.reshape(experts * shards, slot_cap, features)
    arrived = lax.all_to_all(copies, ("exp", "shard"), split_axis=0, concat_axis=0, tiled=True)
    partial_grad = lax.dot_general(
        arrived.reshape(-1, features), cotangent, contract_rows, preferred_element_type=jnp.float32
    )
    weight_grad = lax.psum(partial_grad.astype(jnp.bfloat16), "rep")[None]
    ordered = jnp.swapaxes(blocks, 0, 1).reshape(-1, hidden)
    summed = lax.psum_scatter(
        lax.dot_general(
            ordered, weight, (((1,), (1,)), ((), ())), preferred_element_type=jnp.float32
        ).astype(jnp.bfloat16),
        "shard",
        scatter_dimension=0,
        tiled=True,
    )
    slot_grad = summed.reshape(experts, slot_cap, features)
    returned = lax.all_to_all(slot_grad, "exp", split_axis=0, concat_axis=0, tiled=True)
    token_grad = jnp.dot(
        placing.T, returned.reshape(-1, features), preferred_element_type=jnp.float32
    )
    return (token_grad.astype(jnp.bfloat16), weight_grad)


def solution(mesh):
    placed = (
        P(("rep", "exp", "shard"), None),
        P(("rep", "exp", "shard"), None),
        P("exp", None, "shard"),
        P("exp", "rep", "shard"),
    )
    return jax.shard_map(
        body,
        mesh=mesh,
        in_specs=placed,
        out_specs=(P(("rep", "exp", "shard"), None), P("exp", None, "shard")),
        check_vma=False,
    )
```

profile of v0, /device:TPU:0, one launch (start us, length us, event | category | flops | bytes accessed | tf_op | source)
XLA Modules:
  0.0 571.3 jit_solution(2415380312625847076)
XLA Ops:
  7.2 0.8 copy.16
  8.1 0.1 eq.37
  8.2 1.2 reduce-window.6
  9.5 0.1 slice.12
  9.5 0.1 copy.17
  9.7 0.1 copy.18
  9.8 0.1 add_bitcast_fusion
  9.9 0.1 add.15
  10.0 0.1 copy.19
  10.1 0.1 convert_reduce_fusion
  10.2 0.5 convolution_convert_fusion.1
  10.7 0.3 broadcast_in_dim.6
  11.0 0.2 broadcast_in_dim.7
  11.2 30.7 %all_to_all.10 = bf16[8,63,2048]{2,1,0:T(8,128)(2,1)S(1)} all-to-all(bf16[8,63,2048]{2,1,0:T(8,128)(2,1)S(1)} %bitcast.29), channel_id=1, replica_groups=mesh['rep'=4,'exp'=4,'shard'=2] {'exp','shard'}, dimensions={0} | all-to-all | bytes 4128768 | tf_op jit(solution)/shard_map/all_to_all | solution.py:34
  41.9 2.0 reshape.61
  43.8 13.3 %fusion.3 = bf16[1,2048,3584]{2,1,0:T(8,128)(2,1)} fusion(bf16[504,2048]{1,0:T(8,128)(2,1)} %reshape.61, bf16[1,504,3584]{2,1,0:T(8,128)(2,1)} %param.7), kind=kOutput, calls=%fused_computation.3 | convolution fusion | flops 7406092288 | bytes 20357120 | tf_op jit(solution)/shard_map/dot_general | solution.py:35
  57.2 4.9 reshape_squeeze.3
  62.1 5.2 copy.20
  67.2 4.9 reshape.57
  72.2 13.0 %fusion.5 = bf16[504,2048]{1,0:T(8,128)(2,1)} fusion(bf16[504,3584]{1,0:T(8,128)(2,1)} %reshape.57, bf16[1,2048,3584]{2,1,0:T(8,128)(2,1)} %param.6), kind=kOutput, calls=%fused_computation.5 | convolution fusion | flops 7399784448 | bytes 20357120 | tf_op jit(solution)/shard_map/dot_general | solution.py:41
  85.2 28.6 %fusion = bf16[256,2048]{1,0:T(8,128)(2,1)S(1)} fusion(bf16[504,2048]{1,0:T(8,128)(2,1)} %fusion.5), kind=kCustom, calls=%all-reduce-scatter | all-reduce-scatter fusion | flops 1048577 | bytes 3113472
  113.8 3.6 collective-permute-start
  117.5 0.6 dynamic-slice.4
  118.7 0.2 collective-permute-done
  118.9 1.2 concatenate
  120.1 0.3 constant_dynamic-slice_fusion
  120.4 0.3 reshape.58
  120.7 17.6 %all_to_all.11 = bf16[4,63,2048]{2,1,0:T(8,128)(2,1)} all-to-all(bf16[4,63,2048]{2,1,0:T(8,128)(2,1)S(1)} %reshape.58), channel_id=1, replica_groups=mesh['rep'=4,'exp'=4,'shard'=2] {'exp'}, dimensions={0} | all-to-all | bytes 2064384 | tf_op jit(solution)/shard_map/all_to_all | solution.py:49
  138.3 1.5 reshape.59
  139.8 1.1 convolution_convert_fusion.2
  140.9 410.5 %all-reduce.5.cloned.1.call-done = bf16[1,2048,3584]{2,1,0:T(8,128)(2,1)} async-done(((bf16[1,2048,3584]{2,1,0:T(8,128)(2,1)}), bf16[1,2048,3584]{2,1,0:T(8,128)(2,1)}) %all-reduce.5.cloned.1.call-update) | async-done | bytes 14680080 | tf_op jit(solution)/shard_map/psum | solution.py:38
  551.3 13.2 %copy.25 = bf16[1,2048,3584]{2,1,0:T(8,128)(2,1)} copy(bf16[1,2048,3584]{2,1,0:T(8,128)(2,1)} %all-reduce.5.cloned.1.call-done) | data formatting | bytes 29360128
  (17 shorter events, 0.2 us)
Async XLA Ops:
  7.2 3.1 copy-start
  7.2 544.1 %all-reduce.5.cloned.1.call-start = ((), (), s32[]{:S(2)}) async-start(), calls=%async_computation.2 | async-start | bytes 29360128 | tf_op jit(solution)/shard_map/psum | solution.py:38
  72.2 45.3 %copy-start.2 = (u32[32]{0:T(128)S(1)}, u32[32]{0:T(128)}, u32[]{:S(2)}) copy-start(u32[32]{0:T(128)} %constant.19) | copy-start | bytes 388
  113.8 5.1 collective-permute-start
  551.3 13.2 %copy-start.1 = (bf16[112,2048]{1,0:T(8,128)(2,1)S(1)}, bf16[112,2048]{1,0:T(8,128)(2,1)}, u32[]{:S(2)}) copy-start(bf16[112,2048]{1,0:T(8,128)(2,1)} %param.4) | copy-start | bytes 1376260
Sparse Core Ops, SparseCore 0:
  57.3 493.9 all-reduce.4
where the time goes:
time: 572 us; the launch traced here: 571 us
  waiting for transfers between devices  411 us (72%)
  blocking collectives  76.8 us (13%)
  local copies, waits for them, and re-layouts  36 us (6%)
  matrix products  27.9 us (5%)
  between operations  14.8 us (3%)
    psum x1, waiting for transfers between devices, body(): weight_grad = lax.psum(partial_grad.astype(jnp.bfloat16), 'rep')[None]  410 us
    all_to_all x1, blocking collectives, body(): lax.all_to_all(copies, ('exp', 'shard'), split_axis=0, concat_axis=0, til...  30.7 us
    unnamed x1, blocking collectives  28.6 us
    all_to_all x1, blocking collectives, body(): lax.all_to_all(slot_grad, 'exp', split_axis=0, concat_axis=0, tiled=True)  17.6 us
    unnamed x13, local copies, waits for them, and re-layouts  16.1 us
    dot_general x1, matrix products, body(): lax.dot_general(arrived.reshape(-1, features), cotangent, contract_rows,...  13.3 us
    dot_general x1, matrix products, body(): lax.dot_general(ordered, weight, (((1,), (1,)), ((), ())), preferred_elem...  13 us
  transfers between devices with their start and end apart: 2, of which 2 were waited for; matrix products, arithmetic and copies ran while one was open for 11% of the time, Pallas kernels for 0%

commit v1 on v0

v1 whole, which is shorter than its diff:
```python
import functools

import jax
import jax.numpy as jnp
from jax import lax
from jax.experimental import pallas as pl
from jax.experimental.pallas import tpu as pltpu
from jax.sharding import PartitionSpec as P


ROW_TILE = 256
BOUNDS = (0, 2, 4, 6, 7)


def slot_matrix(route_rows, experts, slot_cap):
    expert_ids = jnp.arange(experts, dtype=jnp.int32)
    onehot = (route_rows[:, :, None] == expert_ids[None, None, :]).astype(jnp.int32)
    named = onehot.sum(axis=1)
    rows = named.shape[0]
    earlier = (jnp.arange(rows)[:, None] > jnp.arange(rows)[None, :]).astype(jnp.bfloat16)
    before = jnp.dot(earlier, named.astype(jnp.bfloat16), preferred_element_type=jnp.float32)
    position = jnp.where(named > 0, before.astype(jnp.int32), -1)
    slot_ids = jnp.arange(slot_cap, dtype=jnp.int32)
    matches = position.T[:, None, :] == slot_ids[None, :, None]
    return matches.reshape(experts * slot_cap, rows).astype(jnp.bfloat16)


def shifted(value, axis, amount):
    size = lax.axis_size(axis)
    return lax.ppermute(value, axis, [(i, (i + amount) % size) for i in range(size)])


def ring_blocks(value):
    size = lax.axis_size("rep")
    up, down, blocks = value, value, [value]
    for _ in range((size - 1) // 2):
        up, down = shifted(up, "rep", 1), shifted(down, "rep", -1)
        blocks += [up, down]
    if size % 2 == 0:
        half = -(-value.shape[0] // 32) * 16
        blocks.append(shifted(up[:half], "rep", 1))
        blocks.append(shifted(down[half:], "rep", -1))
    return blocks


def back_offsets(size):
    offsets = [0]
    for distance in range(1, (size - 1) // 2 + 1):
        offsets += [distance, -distance]
    if size % 2 == 0:
        offsets.append(size // 2)
    return offsets


def grad_kernel(count, tokens_ref, *refs):
    out_ref = refs[-1]
    total, row = None, 0
    for block_ref in refs[:count]:
        rows = block_ref.shape[0]
        term = lax.dot_general(
            tokens_ref[row:row + rows, :], block_ref[...], (((0,), (0,)), ((), ())),
            preferred_element_type=jnp.float32,
        )
        total = term if total is None else total + term
        row += rows
    out_ref[...] = total.astype(out_ref.dtype)


def grad_chunk(gathered, blocks, previous, lower, hidden):
    rows, features = gathered.shape
    width = blocks[0].shape[1]
    count = len(blocks)
    in_specs = [pl.BlockSpec((rows, ROW_TILE), lambda i: (0, i))]
    in_specs += [pl.BlockSpec(b.shape, lambda i: (0, 0)) for b in blocks]
    operands, aliases = [gathered, *blocks], {}
    if previous is not None:
        in_specs.append(pl.BlockSpec(memory_space=pl.ANY))
        operands.append(previous)
        aliases = {count + 1: 0}
    place = lower // width
    return pl.pallas_call(
        functools.partial(grad_kernel, count),
        grid=(features // ROW_TILE,),
        in_specs=in_specs,
        out_specs=pl.BlockSpec((ROW_TILE, width), lambda i: (i, place)),
        out_shape=jax.ShapeDtypeStruct((features, hidden), jnp.bfloat16),
        input_output_aliases=aliases,
        compiler_params=pltpu.CompilerParams(vmem_limit_bytes=48 * 1024 * 1024),
        cost_estimate=pl.CostEstimate(
            flops=2 * rows * features * width,
            bytes_accessed=2 * (rows * (features + width) + features * width),
            transcendentals=0,
        ),
    )(*operands)


def body(tokens, routes, gate_weight, gate_cotangent):
    experts = lax.axis_size("exp")
    shards = lax.axis_size("shard")
    replicas = lax.axis_size("rep")
    features = tokens.shape[1]
    cotangent = gate_cotangent[0]
    hidden = cotangent.shape[1]
    slot_cap = cotangent.shape[0] // (experts * shards)
    weight = gate_weight[0]

    offsets = back_offsets(replicas)
    flat_routes = routes.T
    all_routes = [flat_routes if k == 0 else shifted(flat_routes, "rep", k) for k in offsets]
    all_tokens = [tokens if k == 0 else shifted(tokens, "rep", k) for k in offsets]

    bounds = [hidden * part // 7 for part in BOUNDS]
    chunks = [ring_blocks(cotangent[:, a:b]) for a, b in zip(bounds[:-1], bounds[1:])]

    partial = lax.dot_general(
        cotangent, weight, (((1,), (1,)), ((), ())), preferred_element_type=jnp.float32
    ).astype(jnp.bfloat16)
    partial = partial.reshape(experts, shards, slot_cap, features)
    me = lax.axis_index("shard")
    summed = lax.dynamic_index_in_dim(partial, me, 1, keepdims=False).astype(jnp.float32)
    for k in range(1, shards):
        leaving = lax.dynamic_index_in_dim(partial, (me + k) % shards, 1, keepdims=False)
        summed = summed + shifted(leaving, "shard", k).astype(jnp.float32)
    slot_grad = summed.astype(jnp.bfloat16)
    returned = lax.all_to_all(slot_grad, "exp", split_axis=0, concat_axis=0, tiled=True)
    placings = [slot_matrix(r.T, experts, slot_cap) for r in all_routes]
    token_grad = jnp.dot(
        placings[0].T, returned.reshape(-1, features), preferred_element_type=jnp.float32
    ).astype(jnp.bfloat16)

    outgoing = jnp.stack([
        jnp.dot(p, t, preferred_element_type=jnp.float32).astype(jnp.bfloat16)
        for p, t in zip(placings, all_tokens)
    ])
    outgoing = outgoing.reshape(replicas, experts, 1, slot_cap, features)
    copies = jnp.broadcast_to(outgoing, (replicas, experts, shards, slot_cap, features))
    copies = copies.reshape(replicas, experts * shards, slot_cap, features)
    arrived = lax.all_to_all(copies, ("exp", "shard"), split_axis=1, concat_axis=1, tiled=True)
    gathered = arrived.reshape(-1, features)

    weight_grad = None
    for lower, blocks in zip(bounds[:-1], chunks):
        weight_grad = grad_chunk(gathered, blocks, weight_grad, lower, hidden)
    return (token_grad, weight_grad[None])


def solution(mesh):
    placed = (
        P(("rep", "exp", "shard"), None),
        P(("rep", "exp", "shard"), None),
        P("exp", None, "shard"),
        P("exp", "rep", "shard"),
    )
    return jax.shard_map(
        body,
        mesh=mesh,
        in_specs=placed,
        out_specs=(P(("rep", "exp", "shard"), None), P("exp", None, "shard")),
        check_vma=False,
    )
```

time: 572 us -> 355 us (0.62)
  waiting for transfers between devices: 411 us -> 182 us
  blocking collectives: 76.8 us -> 0 us
  Pallas kernels: 0 us -> 48.6 us
  starting transfers between devices: 3.66 us -> 38.1 us
  local copies, waits for them, and re-layouts: 36 us -> 57.3 us
  between operations: 14.8 us -> 0.92 us
  matrix products: 27.9 us -> 20.6 us
    psum x1 -> x0, waiting for transfers between devices: 410 us -> none  [body(): weight_grad = lax.psum(partial_grad.astype(jnp.bfloat16), 'rep')[None]]
    ppermute x0 -> x23, waiting for transfers between devices: none -> 182 us  [shifted(): lax.ppermute(value, axis, [(i, (i + amount) % size) for i in range(size)])]
    pallas_call x0 -> x4, Pallas kernels: none -> 48.6 us  [grad_chunk(): pl.pallas_call(functools.partial(grad_kernel, count), grid=(features // R...]
    all_to_all x2 -> x0, blocking collectives: 48.2 us -> none  [the longest x1 30.7 us: body(): lax.all_to_all(copies, ('exp', 'shard'), split_axis=0, concat_axis=0, til...]
    ppermute x0 -> x23, starting transfers between devices: none -> 29.4 us  [shifted(): lax.ppermute(value, axis, [(i, (i + amount) % size) for i in range(size)])]
    unnamed x1 -> x0, blocking collectives: 28.6 us -> none
    broadcast_in_dim x2, local copies, waits for them, and re-layouts: 0.52 us -> 11.8 us  [body(): jnp.broadcast_to(outgoing, (replicas, experts, shards, slot_cap, features))]
    all_to_all x0 -> x1, local copies, waits for them, and re-layouts: none -> 11.3 us  [body(): lax.all_to_all(copies, ('exp', 'shard'), split_axis=1, concat_axis=1, til...]
  transfers between devices with their start and end apart: 2 -> 25, of which waited for: 2 -> 11; matrix products, arithmetic and copies ran while one was open for 11% -> 20% of each run, Pallas kernels for 0% -> 11%
where the time goes in v1:
time: 355 us; the launch traced here: 353 us
  waiting for transfers between devices  182 us (51%)
  local copies, waits for them, and re-layouts  57.3 us (16%)
  Pallas kernels  48.6 us (14%)
  starting transfers between devices  38.1 us (11%)
  matrix products  20.6 us (6%)
  other arithmetic  5.71 us (2%)
    ppermute x23, waiting for transfers between devices, shifted(): lax.ppermute(value, axis, [(i, (i + amount) % size) for i in range(size)])  182 us
    pallas_call x4, Pallas kernels, grad_chunk(): pl.pallas_call(functools.partial(grad_kernel, count), grid=(features // R...  48.6 us
    ppermute x23, starting transfers between devices, shifted(): lax.ppermute(value, axis, [(i, (i + amount) % size) for i in range(size)])  29.4 us
    dot_general x1, matrix products, body(): lax.dot_general(cotangent, weight, (((1,), (1,)), ((), ())), preferred_el...  13 us
    broadcast_in_dim x2, local copies, waits for them, and re-layouts, body(): jnp.broadcast_to(outgoing, (replicas, experts, shards, slot_cap, features))  11.8 us
    all_to_all x1, local copies, waits for them, and re-layouts, body(): lax.all_to_all(copies, ('exp', 'shard'), split_axis=1, concat_axis=1, til...  11.3 us
    reshape x1, local copies, waits for them, and re-layouts, body(): gathered = arrived.reshape(-1, features)  7.92 us
  transfers between devices with their start and end apart: 25, of which 11 were waited for; matrix products, arithmetic and copies ran while one was open for 20% of the time, Pallas kernels for 11%

profile of v1, /device:TPU:0, one launch (start us, length us, event | category | flops | bytes accessed | tf_op | source)
XLA Modules:
  0.0 352.8 jit_solution(8285122325177443285)
XLA Ops:
  0.6 3.1 collective-permute-start.1
  5.8 3.8 %collective-permute-start.4 = (bf16[112,2048]{1,0:T(8,128)(2,1)}, bf16[112,2048]{1,0:T(8,128)(2,1)}, u32[]{:S(2)}, u32[]{:S(2)}) collective-permute-start(bf16[112,2048]{1,0:T(8,128)(2,1)} %param.4), channel_id=1, source_target_pairs={{0,24},{8,0},{16,8},{24,16},{1,25},{9,1},{17,9},{25,17},{2,26},{10... | collective-permute-start | bytes 1376264 | tf_op jit(solution)/shard_map/ppermute | solution.py:30
  10.7 13.0 %fusion.2 = bf16[504,2048]{1,0:T(8,128)(2,1)} fusion(bf16[1,2048,3584]{2,1,0:T(8,128)(2,1)} %param.6, bf16[1,504,3584]{2,1,0:T(8,128)(2,1)} %param.7), kind=kOutput, calls=%fused_computation.3 | convolution fusion | flops 7399784448 | bytes 20357120 | tf_op jit(solution)/shard_map/dot_general | solution.py:115
  23.6 2.2 reshape.45
  27.4 2.5 stack.15
  31.7 2.9 collective-permute-start.6
  38.5 19.7 %collective-permute-done = bf16[4,63,2048]{2,0,1:T(4,128)(2,1)} collective-permute-done((bf16[4,63,2048]{2,0,1:T(4,128)(2,1)}, bf16[4,63,2048]{2,0,1:T(4,128)(2,1)}, u32[]{:S(2)}, u32[]{:S(2)}) %collective-permute-start) | collective-permute-done | bytes 1032224 | tf_op jit(solution)/shard_map/ppermute | solution.py:30
  58.2 2.8 fusion.6
  61.0 3.7 %all-to-all-start = ((bf16[4,63,2048]{2,1,0:T(8,128)(2,1)}), bf16[4,63,2048]{2,1,0:T(8,128)(2,1)S(1)}, u32[]{:S(2)}, u32[]{:S(2)}) async-start(bf16[4,63,2048]{2,1,0:T(8,128)(2,1)} %fusion.6), calls=%async_computation | async-start | bytes 2097152 | tf_op jit(solution)/shard_map/all_to_all | solution.py:125
  71.5 2.1 maximum_bitcast_fusion
  73.6 5.2 %copy.39 = bf16[4,4,63,2048]{3,0,2,1:T(4,128)(2,1)} copy(bf16[4,4,63,2048]{3,2,1,0:T(8,128)(2,1)S(1)} %maximum_bitcast_fusion) | data formatting | bytes 8257536 | tf_op jit(solution)/shard_map/broadcast_in_dim | solution.py:136
  78.9 6.7 %broadcast_in_dim.15 = bf16[4,4,2,63,2048]{4,0,3,2,1:T(4,128)(2,1)} broadcast(bf16[4,4,63,2048]{3,0,2,1:T(4,128)(2,1)} %copy.39), dimensions={0,1,3,4} | broadcast | bytes 12386304 | tf_op jit(solution)/shard_map/broadcast_in_dim | solution.py:136
  85.6 4.9 %all-to-all-start.1 = ((bf16[4,8,63,2048]{3,0,2,1:T(4,128)(2,1)}), bf16[4,8,63,2048]{3,0,2,1:T(4,128)(2,1)}, u32[]{:S(2)}, u32[]{:S(2)}) async-start(bf16[4,8,63,2048]{3,0,2,1:T(4,128)(2,1)} %bitcast.41), calls=%async_computation.1 | async-start | bytes 16515072 | tf_op jit(solution)/shard_map/all_to_all | solution.py:138
  90.5 2.2 fusion.25
  94.7 3.4 collective-permute-start.8
  101.0 30.4 %collective-permute-done.7.refs_1_ = bf16[504,512]{1,0:T(8,128)(2,1)S(1)} collective-permute-done((bf16[504,512]{1,0:T(8,128)(2,1)S(1)}, bf16[504,512]{1,0:T(8,128)(2,1)S(1)}, u32[]{:S(2)}, u32[]{:S(2)}) %collective-permute-start.7) | collective-permute-done | bytes 516128 | tf_op jit(solution)/shard_map/ppermute | solution.py:30
  131.4 10.5 %collective-permute-done.8.refs_2_ = bf16[504,512]{1,0:T(8,128)(2,1)S(1)} collective-permute-done((bf16[504,512]{1,0:T(8,128)(2,1)S(1)}, bf16[504,512]{1,0:T(8,128)(2,1)S(1)}, u32[]{:S(2)}, u32[]{:S(2)}) %collective-permute-start.8) | collective-permute-done | bytes 516128 | tf_op jit(solution)/shard_map/ppermute | solution.py:30
  142.5 3.2 collective-permute-start.12
  146.5 18.1 %collective-permute-done.20.refs_2_ = bf16[504,1024]{1,0:T(8,128)(2,1)S(1)} collective-permute-done((bf16[504,1024]{1,0:T(8,128)(2,1)S(1)}, bf16[504,1024]{1,0:T(8,128)(2,1)S(1)}, u32[]{:S(2)}, u32[]{:S(2)}) %collective-permute-start.20) | collective-permute-done | bytes 1032224 | tf_op jit(solution)/shard_map/ppermute | solution.py:30
  166.0 20.7 %collective-permute-done.15.refs_1_ = bf16[504,1024]{1,0:T(8,128)(2,1)S(1)} collective-permute-done((bf16[504,1024]{1,0:T(8,128)(2,1)S(1)}, bf16[504,1024]{1,0:T(8,128)(2,1)S(1)}, u32[]{:S(2)}, u32[]{:S(2)}) %collective-permute-start.15) | collective-permute-done | bytes 1032224 | tf_op jit(solution)/shard_map/ppermute | solution.py:30
  189.0 19.8 %collective-permute-done.16.refs_2_ = bf16[504,1024]{1,0:T(8,128)(2,1)S(1)} collective-permute-done((bf16[504,1024]{1,0:T(8,128)(2,1)S(1)}, bf16[504,1024]{1,0:T(8,128)(2,1)S(1)}, u32[]{:S(2)}, u32[]{:S(2)}) %collective-permute-start.16) | collective-permute-done | bytes 1032224 | tf_op jit(solution)/shard_map/ppermute | solution.py:30
  210.2 20.8 %collective-permute-done.11.refs_1_ = bf16[504,1024]{1,0:T(8,128)(2,1)S(1)} collective-permute-done((bf16[504,1024]{1,0:T(8,128)(2,1)S(1)}, bf16[504,1024]{1,0:T(8,128)(2,1)S(1)}, u32[]{:S(2)}, u32[]{:S(2)}) %collective-permute-start.11) | collective-permute-done | bytes 1032224 | tf_op jit(solution)/shard_map/ppermute | solution.py:30
  231.9 21.0 %collective-permute-done.12.refs_2_ = bf16[504,1024]{1,0:T(8,128)(2,1)S(1)} collective-permute-done((bf16[504,1024]{1,0:T(8,128)(2,1)S(1)}, bf16[504,1024]{1,0:T(8,128)(2,1)S(1)}, u32[]{:S(2)}, u32[]{:S(2)}) %collective-permute-start.12) | collective-permute-done | bytes 1032224 | tf_op jit(solution)/shard_map/ppermute | solution.py:30
  256.6 11.3 %copy.40 = bf16[4,8,63,2048]{3,2,1,0:T(8,128)(2,1)} copy(bf16[4,8,63,2048]{3,0,2,1:T(4,128)(2,1)} %all-to-all-done.1) | data formatting | bytes 16515072 | tf_op jit(solution)/shard_map/all_to_all | solution.py:138
  267.9 7.9 %reshape.47.tokens_ref = bf16[2016,2048]{1,0:T(8,128)(2,1)} reshape(bf16[4,8,63,2048]{3,2,1,0:T(8,128)(2,1)} %copy.40) | data formatting | bytes 16515072 | tf_op jit(solution)/shard_map/reshape | solution.py:139
  275.8 3.2 collective-permute-start.18
  282.7 13.1 %shard_map.59.refs_5_ = bf16[2048,3584]{1,0:T(8,128)(2,1)} custom-call(bf16[2016,2048]{1,0:T(8,128)(2,1)} %reshape.47.tokens_ref, bf16[504,1024]{1,0:T(8,128)(2,1)S(1)} %copy-done.13, bf16[504,1024]{1,0:T(8,128)(2,1)S(1)} %copy-done.15, bf16[504,1024]{1,0:T(8,128)(2,1)S(1)} %copy-done.17, bf16[256,1024]{1,0:T(8,128)(2,1)} %collective-permute-done.21.refs_3_, ...), custom_call_target="tpu_custom_call" | custom-call | flops 8455716864 | bytes 16580608 | tf_op jit(solution)/shard_map/pallas_call | solution.py:81
  295.8 11.9 %collective-permute-done.18.refs_4_ = bf16[248,1024]{1,0:T(8,128)(2,1)S(1)} collective-permute-done((bf16[248,1024]{1,0:T(8,128)(2,1)}, bf16[248,1024]{1,0:T(8,128)(2,1)S(1)}, u32[]{:S(2)}, u32[]{:S(2)}) %collective-permute-start.18) | collective-permute-done | bytes 507936 | tf_op jit(solution)/shard_map/ppermute | solution.py:30
  308.5 12.9 %shard_map.60.refs_5_ = bf16[2048,3584]{1,0:T(8,128)(2,1)} custom-call(bf16[2016,2048]{1,0:T(8,128)(2,1)} %reshape.47.tokens_ref, bf16[504,1024]{1,0:T(8,128)(2,1)S(1)} %get-tuple-element.3.refs_0_, bf16[504,1024]{1,0:T(8,128)(2,1)S(1)} %collective-permute-done.15.refs_1_, bf16[504,1024]{1,0:T(8,128)(2,1)S(1)} %copy-done.3, ...), custom_call_target="tpu_custom_call", output_to_operand_aliasing={{}: (6, {})} | custom-call | flops 8455716864 | bytes 16580608 | tf_op jit(solution)/shard_map/pallas_call | solution.py:81
  321.4 8.7 %collective-permute-done.14.refs_4_ = bf16[248,1024]{1,0:T(8,128)(2,1)S(1)} collective-permute-done((bf16[248,1024]{1,0:T(8,128)(2,1)S(1)}, bf16[248,1024]{1,0:T(8,128)(2,1)S(1)}, u32[]{:S(2)}, u32[]{:S(2)}) %collective-permute-start.14) | collective-permute-done | bytes 507936 | tf_op jit(solution)/shard_map/ppermute | solution.py:30
  330.1 12.7 %shard_map.61.refs_5_ = bf16[2048,3584]{1,0:T(8,128)(2,1)} custom-call(bf16[2016,2048]{1,0:T(8,128)(2,1)} %reshape.47.tokens_ref, bf16[504,1024]{1,0:T(8,128)(2,1)S(1)} %get-tuple-element.4.refs_0_, bf16[504,1024]{1,0:T(8,128)(2,1)S(1)} %copy-done.1, bf16[504,1024]{1,0:T(8,128)(2,1)S(1)} %copy-done.5, ...), custom_call_target="tpu_custom_call", output_to_operand_aliasing={{}: (6, {})} | custom-call | flops 8455716864 | bytes 16580608 | tf_op jit(solution)/shard_map/pallas_call | solution.py:81
  342.8 9.9 %shard_map.62 = bf16[2048,3584]{1,0:T(8,128)(2,1)} custom-call(bf16[2016,2048]{1,0:T(8,128)(2,1)} %reshape.47.tokens_ref, bf16[504,512]{1,0:T(8,128)(2,1)S(1)} %copy-done.7, bf16[504,512]{1,0:T(8,128)(2,1)S(1)} %copy-done.9, bf16[504,512]{1,0:T(8,128)(2,1)S(1)} %copy-done.11, ...), custom_call_target="tpu_custom_call", output_to_operand_aliasing={{}: (6, {})} | custom-call | flops 4227858432 | bytes 12419072 | tf_op jit(solution)/shard_map/pallas_call | solution.py:81
  (115 shorter events, 37.6 us)
Async XLA Ops:
  0.6 31.1 %collective-permute-start.1 = (s32[2,112]{1,0:T(2,128)}, s32[2,112]{1,0:T(2,128)S(1)}, u32[]{:S(2)}, u32[]{:S(2)}) collective-permute-start(s32[2,112]{1,0:T(2,128)} %bitcast.44), channel_id=1, source_target_pairs={{0,8},{8,16},{16,24},{24,0},{1,9},{9,17},{17,25},{25,1},{2,10},{10... | collective-permute-start | bytes 2696 | tf_op jit(solution)/shard_map/ppermute | solution.py:30
  3.7 30.9 %collective-permute-start.3 = (s32[2,112]{1,0:T(2,128)}, s32[2,112]{1,0:T(2,128)S(1)}, u32[]{:S(2)}, u32[]{:S(2)}) collective-permute-start(s32[2,112]{1,0:T(2,128)} %bitcast.45), channel_id=1, source_target_pairs={{0,24},{8,0},{16,8},{24,16},{1,25},{9,1},{17,9},{25,17},{2,26},{10... | collective-permute-start | bytes 2696 | tf_op jit(solution)/shard_map/ppermute | solution.py:30
  5.8 31.1 %collective-permute-start.2 = (bf16[112,2048]{1,0:T(8,128)(2,1)}, bf16[112,2048]{1,0:T(8,128)(2,1)}, u32[]{:S(2)}, u32[]{:S(2)}) collective-permute-start(bf16[112,2048]{1,0:T(8,128)(2,1)} %param.4), channel_id=1, source_target_pairs={{0,8},{8,16},{16,24},{24,0},{1,9},{9,17},{17,25},{25,1},{2,10},{10... | collective-permute-start | bytes 1376264 | tf_op jit(solution)/shard_map/ppermute | solution.py:30
  5.8 58.9 %collective-permute-start.4 = (bf16[112,2048]{1,0:T(8,128)(2,1)}, bf16[112,2048]{1,0:T(8,128)(2,1)}, u32[]{:S(2)}, u32[]{:S(2)}) collective-permute-start(bf16[112,2048]{1,0:T(8,128)(2,1)} %param.4), channel_id=1, source_target_pairs={{0,24},{8,0},{16,8},{24,16},{1,25},{9,1},{17,9},{25,17},{2,26},{10... | collective-permute-start | bytes 1376264 | tf_op jit(solution)/shard_map/ppermute | solution.py:30
  9.7 27.1 %collective-permute-start.5 = (s32[2,112]{1,0:T(2,128)}, s32[2,112]{1,0:T(2,128)S(1)}, u32[]{:S(2)}, u32[]{:S(2)}) collective-permute-start(s32[2,112]{1,0:T(2,128)} %bitcast.46), channel_id=1, source_target_pairs={{0,16},{8,24},{16,0},{24,8},{1,17},{9,25},{17,1},{25,9},{2,18},{10... | collective-permute-start | bytes 2696 | tf_op jit(solution)/shard_map/ppermute | solution.py:30
  31.7 37.0 %collective-permute-start.6 = (bf16[112,2048]{1,0:T(8,128)(2,1)}, bf16[112,2048]{1,0:T(8,128)(2,1)}, u32[]{:S(2)}, u32[]{:S(2)}) collective-permute-start(bf16[112,2048]{1,0:T(8,128)(2,1)} %param.4), channel_id=1, source_target_pairs={{0,16},{8,24},{16,0},{24,8},{1,17},{9,25},{17,1},{25,9},{2,18},{10... | collective-permute-start | bytes 1376264 | tf_op jit(solution)/shard_map/ppermute | solution.py:30
  34.6 23.5 %collective-permute-start = (bf16[4,63,2048]{2,0,1:T(4,128)(2,1)}, bf16[4,63,2048]{2,0,1:T(4,128)(2,1)}, u32[]{:S(2)}, u32[]{:S(2)}) collective-permute-start(bf16[4,63,2048]{2,0,1:T(4,128)(2,1)} %copy.37), channel_id=1, source_target_pairs={{0,1},{1,0},{2,3},{3,2},{4,5},{5,4},{6,7},{7,6},{8,9},{9,8},{10,11... | collective-permute-start | bytes 3096584 | tf_op jit(solution)/shard_map/ppermute | solution.py:30
  61.0 17.9 %all-to-all-start = ((bf16[4,63,2048]{2,1,0:T(8,128)(2,1)}), bf16[4,63,2048]{2,1,0:T(8,128)(2,1)S(1)}, u32[]{:S(2)}, u32[]{:S(2)}) async-start(bf16[4,63,2048]{2,1,0:T(8,128)(2,1)} %fusion.6), calls=%async_computation | async-start | bytes 2097152 | tf_op jit(solution)/shard_map/all_to_all | solution.py:125
  85.6 171.0 %all-to-all-start.1 = ((bf16[4,8,63,2048]{3,0,2,1:T(4,128)(2,1)}), bf16[4,8,63,2048]{3,0,2,1:T(4,128)(2,1)}, u32[]{:S(2)}, u32[]{:S(2)}) async-start(bf16[4,8,63,2048]{3,0,2,1:T(4,128)(2,1)} %bitcast.41), calls=%async_computation.1 | async-start | bytes 16515072 | tf_op jit(solution)/shard_map/all_to_all | solution.py:138
  92.7 161.7 %copy-start.12 = (bf16[504,1024]{1,0:T(8,128)(2,1)}, bf16[504,1024]{1,0:T(8,128)(2,1)S(1)}, u32[]{:S(2)}) copy-start(bf16[504,1024]{1,0:T(8,128)(2,1)S(1)} %get-tuple-element.2.refs_0_) | copy-start | bytes 3096580
  92.7 162.7 %copy-start.19 = (bf16[4,63,2048]{2,1,0:T(8,128)(2,1)S(1)}, bf16[4,63,2048]{2,1,0:T(8,128)(2,1)}, u32[]{:S(2)}) copy-start(bf16[4,63,2048]{2,1,0:T(8,128)(2,1)} %copy-done.18) | copy-start | bytes 3096580
  92.7 49.8 %collective-permute-start.19 = (bf16[504,1024]{1,0:T(8,128)(2,1)S(1)}, bf16[504,1024]{1,0:T(8,128)(2,1)S(1)}, u32[]{:S(2)}, u32[]{:S(2)}) collective-permute-start(bf16[504,1024]{1,0:T(8,128)(2,1)S(1)} %get-tuple-element.2.refs_0_), channel_id=1, source_target_pairs={{0,8},{8,16},{16,24},{24,0},{1,9},{9,17},{17,25},{25,1},{2,10},{10... | collective-permute-start | bytes 3096584 | tf_op jit(solution)/shard_map/ppermute | solution.py:30
  94.3 37.1 %collective-permute-start.7 = (bf16[504,512]{1,0:T(8,128)(2,1)S(1)}, bf16[504,512]{1,0:T(8,128)(2,1)S(1)}, u32[]{:S(2)}, u32[]{:S(2)}) collective-permute-start(bf16[504,512]{1,0:T(8,128)(2,1)S(1)} %slice.48.refs_0_), channel_id=1, source_target_pairs={{0,8},{8,16},{16,24},{24,0},{1,9},{9,17},{17,25},{25,1},{2,10},{10... | collective-permute-start | bytes 1548296 | tf_op jit(solution)/shard_map/ppermute | solution.py:30
  94.7 47.1 %collective-permute-start.8 = (bf16[504,512]{1,0:T(8,128)(2,1)S(1)}, bf16[504,512]{1,0:T(8,128)(2,1)S(1)}, u32[]{:S(2)}, u32[]{:S(2)}) collective-permute-start(bf16[504,512]{1,0:T(8,128)(2,1)S(1)} %slice.48.refs_0_), channel_id=1, source_target_pairs={{0,24},{8,0},{16,8},{24,16},{1,25},{9,1},{17,9},{25,17},{2,26},{10... | collective-permute-start | bytes 1548296 | tf_op jit(solution)/shard_map/ppermute | solution.py:30
  98.9 65.6 %collective-permute-start.20 = (bf16[504,1024]{1,0:T(8,128)(2,1)S(1)}, bf16[504,1024]{1,0:T(8,128)(2,1)S(1)}, u32[]{:S(2)}, u32[]{:S(2)}) collective-permute-start(bf16[504,1024]{1,0:T(8,128)(2,1)S(1)} %get-tuple-element.2.refs_0_), channel_id=1, source_target_pairs={{0,24},{8,0},{16,8},{24,16},{1,25},{9,1},{17,9},{25,17},{2,26},{10... | collective-permute-start | bytes 3096584 | tf_op jit(solution)/shard_map/ppermute | solution.py:30
  100.5 86.2 %collective-permute-start.15 = (bf16[504,1024]{1,0:T(8,128)(2,1)S(1)}, bf16[504,1024]{1,0:T(8,128)(2,1)S(1)}, u32[]{:S(2)}, u32[]{:S(2)}) collective-permute-start(bf16[504,1024]{1,0:T(8,128)(2,1)S(1)} %get-tuple-element.3.refs_0_), channel_id=1, source_target_pairs={{0,8},{8,16},{16,24},{24,0},{1,9},{9,17},{17,25},{25,1},{2,10},{10... | collective-permute-start | bytes 3096584 | tf_op jit(solution)/shard_map/ppermute | solution.py:30
  131.4 123.0 %copy-start.8 = (bf16[504,512]{1,0:T(8,128)(2,1)}, bf16[504,512]{1,0:T(8,128)(2,1)S(1)}, u32[]{:S(2)}) copy-start(bf16[504,512]{1,0:T(8,128)(2,1)S(1)} %collective-permute-done.7.refs_1_) | copy-start | bytes 1548292
  131.4 77.4 %collective-permute-start.16 = (bf16[504,1024]{1,0:T(8,128)(2,1)S(1)}, bf16[504,1024]{1,0:T(8,128)(2,1)S(1)}, u32[]{:S(2)}, u32[]{:S(2)}) collective-permute-start(bf16[504,1024]{1,0:T(8,128)(2,1)S(1)} %get-tuple-element.3.refs_0_), channel_id=1, source_target_pairs={{0,24},{8,0},{16,8},{24,16},{1,25},{9,1},{17,9},{25,17},{2,26},{10... | collective-permute-start | bytes 3096584 | tf_op jit(solution)/shard_map/ppermute | solution.py:30
  141.9 112.5 %copy-start.10 = (bf16[504,512]{1,0:T(8,128)(2,1)}, bf16[504,512]{1,0:T(8,128)(2,1)S(1)}, u32[]{:S(2)}) copy-start(bf16[504,512]{1,0:T(8,128)(2,1)S(1)} %collective-permute-done.8.refs_2_) | copy-start | bytes 1548292
  141.9 89.1 %collective-permute-start.11 = (bf16[504,1024]{1,0:T(8,128)(2,1)S(1)}, bf16[504,1024]{1,0:T(8,128)(2,1)S(1)}, u32[]{:S(2)}, u32[]{:S(2)}) collective-permute-start(bf16[504,1024]{1,0:T(8,128)(2,1)S(1)} %get-tuple-element.4.refs_0_), channel_id=1, source_target_pairs={{0,8},{8,16},{16,24},{24,0},{1,9},{9,17},{17,25},{25,1},{2,10},{10... | collective-permute-start | bytes 3096584 | tf_op jit(solution)/shard_map/ppermute | solution.py:30
  142.5 112.0 %copy-start.14 = (bf16[504,1024]{1,0:T(8,128)(2,1)}, bf16[504,1024]{1,0:T(8,128)(2,1)S(1)}, u32[]{:S(2)}) copy-start(bf16[504,1024]{1,0:T(8,128)(2,1)S(1)} %collective-permute-done.19.refs_1_) | copy-start | bytes 3096580
  142.5 110.5 %collective-permute-start.12 = (bf16[504,1024]{1,0:T(8,128)(2,1)S(1)}, bf16[504,1024]{1,0:T(8,128)(2,1)S(1)}, u32[]{:S(2)}, u32[]{:S(2)}) collective-permute-start(bf16[504,1024]{1,0:T(8,128)(2,1)S(1)} %get-tuple-element.4.refs_0_), channel_id=1, source_target_pairs={{0,24},{8,0},{16,8},{24,16},{1,25},{9,1},{17,9},{25,17},{2,26},{10... | collective-permute-start | bytes 3096584 | tf_op jit(solution)/shard_map/ppermute | solution.py:30
  164.6 89.8 %copy-start.16 = (bf16[504,1024]{1,0:T(8,128)(2,1)}, bf16[504,1024]{1,0:T(8,128)(2,1)S(1)}, u32[]{:S(2)}) copy-start(bf16[504,1024]{1,0:T(8,128)(2,1)S(1)} %collective-permute-done.20.refs_2_) | copy-start | bytes 3096580
  164.6 114.4 %collective-permute-start.21 = (bf16[256,1024]{1,0:T(8,128)(2,1)}, bf16[256,1024]{1,0:T(8,128)(2,1)}, u32[]{:S(2)}, u32[]{:S(2)}) collective-permute-start(bf16[256,1024]{1,0:T(8,128)(2,1)} %slice.58), channel_id=1, source_target_pairs={{0,8},{8,16},{16,24},{24,0},{1,9},{9,17},{17,25},{25,1},{2,10},{10... | collective-permute-start | bytes 1572872 | tf_op jit(solution)/shard_map/ppermute | solution.py:30
  186.7 89.1 %collective-permute-start.22 = (bf16[248,1024]{1,0:T(8,128)(2,1)}, bf16[248,1024]{1,0:T(8,128)(2,1)}, u32[]{:S(2)}, u32[]{:S(2)}) collective-permute-start(bf16[248,1024]{1,0:T(8,128)(2,1)} %slice.59), channel_id=1, source_target_pairs={{0,24},{8,0},{16,8},{24,16},{1,25},{9,1},{17,9},{25,17},{2,26},{10... | collective-permute-start | bytes 1523720 | tf_op jit(solution)/shard_map/ppermute | solution.py:30
  208.8 44.8 %copy-start.2 = (bf16[504,1024]{1,0:T(8,128)(2,1)}, bf16[504,1024]{1,0:T(8,128)(2,1)S(1)}, u32[]{:S(2)}) copy-start(bf16[504,1024]{1,0:T(8,128)(2,1)S(1)} %collective-permute-done.16.refs_2_) | copy-start | bytes 3096580
  208.8 134.0 %collective-permute-start.9 = (bf16[256,512]{1,0:T(8,128)(2,1)}, bf16[256,512]{1,0:T(8,128)(2,1)S(1)}, u32[]{:S(2)}, u32[]{:S(2)}) collective-permute-start(bf16[256,512]{1,0:T(8,128)(2,1)} %slice.49), channel_id=1, source_target_pairs={{0,8},{8,16},{16,24},{24,0},{1,9},{9,17},{17,25},{25,1},{2,10},{10... | collective-permute-start | bytes 786440 | tf_op jit(solution)/shard_map/ppermute | solution.py:30
  231.0 111.8 %collective-permute-start.10 = (bf16[248,512]{1,0:T(8,128)(2,1)}, bf16[248,512]{1,0:T(8,128)(2,1)}, u32[]{:S(2)}, u32[]{:S(2)}) collective-permute-start(bf16[248,512]{1,0:T(8,128)(2,1)} %slice.50), channel_id=1, source_target_pairs={{0,24},{8,0},{16,8},{24,16},{1,25},{9,1},{17,9},{25,17},{2,26},{10... | collective-permute-start | bytes 761864 | tf_op jit(solution)/shard_map/ppermute | solution.py:30
  253.0 55.6 %collective-permute-start.17 = (bf16[256,1024]{1,0:T(8,128)(2,1)}, bf16[256,1024]{1,0:T(8,128)(2,1)}, u32[]{:S(2)}, u32[]{:S(2)}) collective-permute-start(bf16[256,1024]{1,0:T(8,128)(2,1)} %slice.55), channel_id=1, source_target_pairs={{0,8},{8,16},{16,24},{24,0},{1,9},{9,17},{17,25},{25,1},{2,10},{10... | collective-permute-start | bytes 1572872 | tf_op jit(solution)/shard_map/ppermute | solution.py:30
  275.8 31.8 %collective-permute-start.18 = (bf16[248,1024]{1,0:T(8,128)(2,1)}, bf16[248,1024]{1,0:T(8,128)(2,1)S(1)}, u32[]{:S(2)}, u32[]{:S(2)}) collective-permute-start(bf16[248,1024]{1,0:T(8,128)(2,1)} %slice.56), channel_id=1, source_target_pairs={{0,24},{8,0},{16,8},{24,16},{1,25},{9,1},{17,9},{25,17},{2,26},{10... | collective-permute-start | bytes 1523720 | tf_op jit(solution)/shard_map/ppermute | solution.py:30
  279.0 51.1 %collective-permute-start.13 = (bf16[256,1024]{1,0:T(8,128)(2,1)}, bf16[256,1024]{1,0:T(8,128)(2,1)S(1)}, u32[]{:S(2)}, u32[]{:S(2)}) collective-permute-start(bf16[256,1024]{1,0:T(8,128)(2,1)} %slice.52), channel_id=1, source_target_pairs={{0,8},{8,16},{16,24},{24,0},{1,9},{9,17},{17,25},{25,1},{2,10},{10... | collective-permute-start | bytes 1572872 | tf_op jit(solution)/shard_map/ppermute | solution.py:30
  307.6 22.5 %collective-permute-start.14 = (bf16[248,1024]{1,0:T(8,128)(2,1)S(1)}, bf16[248,1024]{1,0:T(8,128)(2,1)S(1)}, u32[]{:S(2)}, u32[]{:S(2)}) collective-permute-start(bf16[248,1024]{1,0:T(8,128)(2,1)S(1)} %copy-done.21), channel_id=1, source_target_pairs={{0,24},{8,0},{16,8},{24,16},{1,25},{9,1},{17,9},{25,17},{2,26},{10... | collective-permute-start | bytes 1523720 | tf_op jit(solution)/shard_map/ppermute | solution.py:30
  (16 other events, 231.0 us)

commit v2 on v1

--- a/solution.py
+++ b/solution.py
@@ -8,7 +8,7 @@
 from jax.sharding import PartitionSpec as P
 
 
-ROW_TILE = 256
+ROW_TILE = 512
 BOUNDS = (0, 2, 4, 6, 7)
 
 
@@ -52,34 +52,36 @@
     return offsets
 
 
-def grad_kernel(count, tokens_ref, *refs):
-    out_ref = refs[-1]
-    total, row = None, 0
-    for block_ref in refs[:count]:
+def grad_kernel(sources, count, *refs):
+    rows_refs, block_refs, out_ref = refs[:sources], refs[sources:sources + count], refs[-1]
+    total, source, row = None, 0, 0
+    for block_ref in block_refs:
         rows = block_ref.shape[0]
         term = lax.dot_general(
-            tokens_ref[row:row + rows, :], block_ref[...], (((0,), (0,)), ((), ())),
+            rows_refs[source][row:row + rows, :], block_ref[...], (((0,), (0,)), ((), ())),
             preferred_element_type=jnp.float32,
         )
         total = term if total is None else total + term
         row += rows
+        if row == rows_refs[source].shape[0]:
+            source, row = source + 1, 0
     out_ref[...] = total.astype(out_ref.dtype)
 
 
 def grad_chunk(gathered, blocks, previous, lower, hidden):
-    rows, features = gathered.shape
+    features = gathered[0].shape[1]
+    rows = sum(g.shape[0] for g in gathered)
     width = blocks[0].shape[1]
-    count = len(blocks)
-    in_specs = [pl.BlockSpec((rows, ROW_TILE), lambda i: (0, i))]
+    in_specs = [pl.BlockSpec((g.shape[0], ROW_TILE), lambda i: (0, i)) for g in gathered]
     in_specs += [pl.BlockSpec(b.shape, lambda i: (0, 0)) for b in blocks]
-    operands, aliases = [gathered, *blocks], {}
+    operands, aliases = [*gathered, *blocks], {}
     if previous is not None:
         in_specs.append(pl.BlockSpec(memory_space=pl.ANY))
+        aliases = {len(operands): 0}
         operands.append(previous)
-        aliases = {count + 1: 0}
     place = lower // width
     return pl.pallas_call(
-        functools.partial(grad_kernel, count),
+        functools.partial(grad_kernel, len(gathered), len(blocks)),
         grid=(features // ROW_TILE,),
         in_specs=in_specs,
         out_specs=pl.BlockSpec((ROW_TILE, width), lambda i: (i, place)),
@@ -128,15 +130,14 @@
         placings[0].T, returned.reshape(-1, features), preferred_element_type=jnp.float32
     ).astype(jnp.bfloat16)
 
-    outgoing = jnp.stack([
-        jnp.dot(p, t, preferred_element_type=jnp.float32).astype(jnp.bfloat16)
-        for p, t in zip(placings, all_tokens)
-    ])
-    outgoing = outgoing.reshape(replicas, experts, 1, slot_cap, features)
-    copies = jnp.broadcast_to(outgoing, (replicas, experts, shards, slot_cap, features))
-    copies = copies.reshape(replicas, experts * shards, slot_cap, features)
-    arrived = lax.all_to_all(copies, ("exp", "shard"), split_axis=1, concat_axis=1, tiled=True)
-    gathered = arrived.reshape(-1, features)
+    gathered = []
+    for placing, rows in zip(placings, all_tokens):
+        outgoing = jnp.dot(placing, rows, preferred_element_type=jnp.float32)
+        outgoing = outgoing.astype(jnp.bfloat16).reshape(experts, 1, slot_cap, features)
+        copies = jnp.broadcast_to(outgoing, (experts, shards, slot_cap, features))
+        copies = copies.reshape(experts * shards, slot_cap, features)
+        arrived = lax.all_to_all(copies, ("exp", "shard"), split_axis=0, concat_axis=0, tiled=True)
+        gathered.append(arrived.reshape(-1, features))
 
     weight_grad = None
     for lower, blocks in zip(bounds[:-1], chunks):

time: 355 us -> 399 us (1.12)
  starting transfers between devices: 38.1 us -> 129 us
  waiting for transfers between devices: 182 us -> 149 us
  local copies, waits for them, and re-layouts: 57.3 us -> 48.1 us
    ppermute x23, starting transfers between devices: 29.4 us -> 107 us  [shifted(): lax.ppermute(value, axis, [(i, (i + amount) % size) for i in range(size)])]
    ppermute x23, waiting for transfers between devices: 182 us -> 139 us  [shifted(): lax.ppermute(value, axis, [(i, (i + amount) % size) for i in range(size)])]
    all_to_all x1 -> x4, starting transfers between devices: 4.93 us -> 17.6 us  [body(): lax.all_to_all(copies, ('exp', 'shard'), split_axis=0, concat_axis=0, til...]
    all_to_all x1 -> x0, local copies, waits for them, and re-layouts: 11.3 us -> none  [body(): lax.all_to_all(copies, ('exp', 'shard'), split_axis=1, concat_axis=1, til...]
    all_to_all x1 -> x4, waiting for transfers between devices: 0.01 us -> 9.6 us  [body(): lax.all_to_all(copies, ('exp', 'shard'), split_axis=0, concat_axis=0, til...]
    another operation x4 -> x0, local copies, waits for them, and re-layouts: 6.27 us -> none  [body(): jnp.stack([jnp.dot(p, t, preferred_element_type=jnp.float32).astype(jnp.b...]
    reshape x1 -> x4, local copies, waits for them, and re-layouts: 7.92 us -> 12.8 us  [body(): gathered.append(arrived.reshape(-1, features))]
    broadcast_in_dim x2 -> x8, local copies, waits for them, and re-layouts: 11.8 us -> 11.5 us  [body(): copies = jnp.broadcast_to(outgoing, (experts, shards, slot_cap, features))]
  transfers between devices with their start and end apart: 25 -> 28, of which waited for: 11 -> 10; matrix products, arithmetic and copies ran while one was open for 20% -> 16% of each run, Pallas kernels for 11% -> 9%
where the time goes in v2:
time: 399 us; the launch traced here: 398 us
  waiting for transfers between devices  149 us (37%)
  starting transfers between devices  129 us (32%)
  local copies, waits for them, and re-layouts  48.1 us (12%)
  Pallas kernels  45.1 us (11%)
  matrix products  21.8 us (5%)
    ppermute x23, waiting for transfers between devices, shifted(): lax.ppermute(value, axis, [(i, (i + amount) % size) for i in range(size)])  139 us
    ppermute x23, starting transfers between devices, shifted(): lax.ppermute(value, axis, [(i, (i + amount) % size) for i in range(size)])  107 us
    pallas_call x4, Pallas kernels, grad_chunk(): pl.pallas_call(functools.partial(grad_kernel, len(gathered), len(blocks))...  45.1 us
    all_to_all x4, starting transfers between devices, body(): lax.all_to_all(copies, ('exp', 'shard'), split_axis=0, concat_axis=0, til...  17.6 us
    dot_general x1, matrix products, body(): lax.dot_general(cotangent, weight, (((1,), (1,)), ((), ())), preferred_el...  13 us
    reshape x4, local copies, waits for them, and re-layouts, body(): gathered.append(arrived.reshape(-1, features))  12.8 us
    broadcast_in_dim x8, local copies, waits for them, and re-layouts, body(): copies = jnp.broadcast_to(outgoing, (experts, shards, slot_cap, features))  11.5 us
    all_to_all x4, waiting for transfers between devices, body(): lax.all_to_all(copies, ('exp', 'shard'), split_axis=0, concat_axis=0, til...  9.6 us
  transfers between devices with their start and end apart: 28, of which 10 were waited for; matrix products, arithmetic and copies ran while one was open for 16% of the time, Pallas kernels for 9%

profile of v2, /device:TPU:0, one launch (start us, length us, event | category | flops | bytes accessed | tf_op | source)
XLA Modules:
  0.0 397.6 jit_solution(1788373532923625540)
XLA Ops:
  5.0 5.2 %all-to-all-start.1 = ((bf16[8,63,2048]{2,1,0:T(8,128)(2,1)}), bf16[8,63,2048]{2,1,0:T(8,128)(2,1)S(1)}, u32[]{:S(2)}, u32[]{:S(2)}) async-start(bf16[8,63,2048]{2,1,0:T(8,128)(2,1)} %bitcast.43), calls=%async_computation.1 | async-start | bytes 4194304 | tf_op jit(solution)/shard_map/all_to_all | solution.py:139
  10.2 13.0 %fusion.2 = bf16[504,2048]{1,0:T(8,128)(2,1)} fusion(bf16[1,2048,3584]{2,1,0:T(8,128)(2,1)} %param.6, bf16[1,504,3584]{2,1,0:T(8,128)(2,1)} %param.7), kind=kOutput, calls=%fused_computation.2 | convolution fusion | flops 7399784448 | bytes 20357120 | tf_op jit(solution)/shard_map/dot_general | solution.py:117
  31.8 26.2 %collective-permute-done = bf16[4,63,2048]{2,0,1:T(4,128)(2,1)S(1)} collective-permute-done((bf16[4,63,2048]{2,0,1:T(4,128)(2,1)}, bf16[4,63,2048]{2,0,1:T(4,128)(2,1)S(1)}, u32[]{:S(2)}, u32[]{:S(2)}) %collective-permute-start) | collective-permute-done | bytes 1032224 | tf_op jit(solution)/shard_map/ppermute | solution.py:30
  60.9 4.4 %all-to-all-start = ((bf16[4,63,2048]{2,1,0:T(8,128)(2,1)}), bf16[4,63,2048]{2,1,0:T(8,128)(2,1)}, u32[]{:S(2)}, u32[]{:S(2)}) async-start(bf16[4,63,2048]{2,1,0:T(8,128)(2,1)} %fusion.6), calls=%async_computation | async-start | bytes 2097152 | tf_op jit(solution)/shard_map/all_to_all | solution.py:127
  68.5 11.6 %collective-permute-done.1 = s32[2,112]{1,0:T(2,128)S(1)} collective-permute-done((s32[2,112]{1,0:T(2,128)S(1)}, s32[2,112]{1,0:T(2,128)S(1)}, u32[]{:S(2)}, u32[]{:S(2)}) %collective-permute-start.1) | collective-permute-done | bytes 928 | tf_op jit(solution)/shard_map/ppermute | solution.py:30
  84.9 3.7 all-to-all-start.2
  90.9 10.6 %collective-permute-done.3 = s32[2,112]{1,0:T(2,128)S(1)} collective-permute-done((s32[2,112]{1,0:T(2,128)S(1)}, s32[2,112]{1,0:T(2,128)S(1)}, u32[]{:S(2)}, u32[]{:S(2)}) %collective-permute-start.3) | collective-permute-done | bytes 928 | tf_op jit(solution)/shard_map/ppermute | solution.py:30
  104.7 9.6 %all-to-all-done.2 = bf16[8,63,2048]{2,1,0:T(8,128)(2,1)S(1)} async-done(((bf16[8,63,2048]{2,1,0:T(8,128)(2,1)}), bf16[8,63,2048]{2,1,0:T(8,128)(2,1)S(1)}, u32[]{:S(2)}, u32[]{:S(2)}) %all-to-all-start.2) | async-done | bytes 2064416 | tf_op jit(solution)/shard_map/all_to_all | solution.py:139
  116.4 4.3 %all-to-all-start.3 = ((bf16[8,63,2048]{2,1,0:T(8,128)(2,1)}), bf16[8,63,2048]{2,1,0:T(8,128)(2,1)}, u32[]{:S(2)}, u32[]{:S(2)}) async-start(bf16[8,63,2048]{2,1,0:T(8,128)(2,1)} %bitcast.44), calls=%async_computation.3 | async-start | bytes 4194304 | tf_op jit(solution)/shard_map/all_to_all | solution.py:139
  125.6 3.8 collective-permute-start.8
  132.8 24.0 %collective-permute-done.6 = bf16[112,2048]{1,0:T(8,128)(2,1)S(1)} collective-permute-done((bf16[112,2048]{1,0:T(8,128)(2,1)S(1)}, bf16[112,2048]{1,0:T(8,128)(2,1)S(1)}, u32[]{:S(2)}, u32[]{:S(2)}) %collective-permute-start.6) | collective-permute-done | bytes 458784 | tf_op jit(solution)/shard_map/ppermute | solution.py:30
  161.4 4.4 %all-to-all-start.4 = ((bf16[8,63,2048]{2,1,0:T(8,128)(2,1)}), bf16[8,63,2048]{2,1,0:T(8,128)(2,1)}, u32[]{:S(2)}, u32[]{:S(2)}) async-start(bf16[8,63,2048]{2,1,0:T(8,128)(2,1)} %bitcast.42), calls=%async_computation.4 | async-start | bytes 4194304 | tf_op jit(solution)/shard_map/all_to_all | solution.py:139
  169.7 12.3 %collective-permute-done.8.refs_6_ = bf16[504,512]{1,0:T(8,128)(2,1)} collective-permute-done((bf16[504,512]{1,0:T(8,128)(2,1)}, bf16[504,512]{1,0:T(8,128)(2,1)}, u32[]{:S(2)}, u32[]{:S(2)}) %collective-permute-start.8) | collective-permute-done | bytes 516128 | tf_op jit(solution)/shard_map/ppermute | solution.py:30
  182.0 8.6 %collective-permute-start.11 = (bf16[504,1024]{1,0:T(8,128)(2,1)S(1)}, bf16[504,1024]{1,0:T(8,128)(2,1)S(1)}, u32[]{:S(2)}, u32[]{:S(2)}) collective-permute-start(bf16[504,1024]{1,0:T(8,128)(2,1)S(1)} %get-tuple-element.4.refs_4_), channel_id=1, source_target_pairs={{0,8},{8,16},{16,24},{24,0},{1,9},{9,17},{17,25},{25,1},{2,10},{10... | collective-permute-start | bytes 3096584 | tf_op jit(solution)/shard_map/ppermute | solution.py:30
  190.6 15.0 %collective-permute-start.12 = (bf16[504,1024]{1,0:T(8,128)(2,1)S(1)}, bf16[504,1024]{1,0:T(8,128)(2,1)S(1)}, u32[]{:S(2)}, u32[]{:S(2)}) collective-permute-start(bf16[504,1024]{1,0:T(8,128)(2,1)S(1)} %get-tuple-element.4.refs_4_), channel_id=1, source_target_pairs={{0,24},{8,0},{16,8},{24,16},{1,25},{9,1},{17,9},{25,17},{2,26},{10... | collective-permute-start | bytes 3096584 | tf_op jit(solution)/shard_map/ppermute | solution.py:30
  207.4 18.7 %collective-permute-done.20.refs_6_ = bf16[504,1024]{1,0:T(8,128)(2,1)S(1)} collective-permute-done((bf16[504,1024]{1,0:T(8,128)(2,1)}, bf16[504,1024]{1,0:T(8,128)(2,1)S(1)}, u32[]{:S(2)}, u32[]{:S(2)}) %collective-permute-start.20) | collective-permute-done | bytes 1032224 | tf_op jit(solution)/shard_map/ppermute | solution.py:30
  226.1 8.6 %collective-permute-start.21 = (bf16[256,1024]{1,0:T(8,128)(2,1)}, bf16[256,1024]{1,0:T(8,128)(2,1)}, u32[]{:S(2)}, u32[]{:S(2)}) collective-permute-start(bf16[256,1024]{1,0:T(8,128)(2,1)} %slice.58), channel_id=1, source_target_pairs={{0,8},{8,16},{16,24},{24,0},{1,9},{9,17},{17,25},{25,1},{2,10},{10... | collective-permute-start | bytes 1572872 | tf_op jit(solution)/shard_map/ppermute | solution.py:30
  235.5 14.2 %collective-permute-start.22 = (bf16[248,1024]{1,0:T(8,128)(2,1)}, bf16[248,1024]{1,0:T(8,128)(2,1)}, u32[]{:S(2)}, u32[]{:S(2)}) collective-permute-start(bf16[248,1024]{1,0:T(8,128)(2,1)} %slice.59), channel_id=1, source_target_pairs={{0,24},{8,0},{16,8},{24,16},{1,25},{9,1},{17,9},{25,17},{2,26},{10... | collective-permute-start | bytes 1523720 | tf_op jit(solution)/shard_map/ppermute | solution.py:30
  253.9 16.5 %collective-permute-done.16.refs_6_ = bf16[504,1024]{1,0:T(8,128)(2,1)S(1)} collective-permute-done((bf16[504,1024]{1,0:T(8,128)(2,1)S(1)}, bf16[504,1024]{1,0:T(8,128)(2,1)S(1)}, u32[]{:S(2)}, u32[]{:S(2)}) %collective-permute-start.16) | collective-permute-done | bytes 1032224 | tf_op jit(solution)/shard_map/ppermute | solution.py:30
  270.4 8.6 %collective-permute-start.9 = (bf16[256,512]{1,0:T(8,128)(2,1)}, bf16[256,512]{1,0:T(8,128)(2,1)S(1)}, u32[]{:S(2)}, u32[]{:S(2)}) collective-permute-start(bf16[256,512]{1,0:T(8,128)(2,1)} %slice.49), channel_id=1, source_target_pairs={{0,8},{8,16},{16,24},{24,0},{1,9},{9,17},{17,25},{25,1},{2,10},{10... | collective-permute-start | bytes 786440 | tf_op jit(solution)/shard_map/ppermute | solution.py:30
  279.8 14.1 %collective-permute-start.10 = (bf16[248,512]{1,0:T(8,128)(2,1)}, bf16[248,512]{1,0:T(8,128)(2,1)}, u32[]{:S(2)}, u32[]{:S(2)}) collective-permute-start(bf16[248,512]{1,0:T(8,128)(2,1)} %slice.50), channel_id=1, source_target_pairs={{0,24},{8,0},{16,8},{24,16},{1,25},{9,1},{17,9},{25,17},{2,26},{10... | collective-permute-start | bytes 761864 | tf_op jit(solution)/shard_map/ppermute | solution.py:30
  294.7 9.0 %collective-permute-done.12.refs_6_ = bf16[504,1024]{1,0:T(8,128)(2,1)S(1)} collective-permute-done((bf16[504,1024]{1,0:T(8,128)(2,1)S(1)}, bf16[504,1024]{1,0:T(8,128)(2,1)S(1)}, u32[]{:S(2)}, u32[]{:S(2)}) %collective-permute-start.12) | collective-permute-done | bytes 1032224 | tf_op jit(solution)/shard_map/ppermute | solution.py:30
  303.7 8.6 %collective-permute-start.17 = (bf16[256,1024]{1,0:T(8,128)(2,1)}, bf16[256,1024]{1,0:T(8,128)(2,1)}, u32[]{:S(2)}, u32[]{:S(2)}) collective-permute-start(bf16[256,1024]{1,0:T(8,128)(2,1)} %slice.55), channel_id=1, source_target_pairs={{0,8},{8,16},{16,24},{24,0},{1,9},{9,17},{17,25},{25,1},{2,10},{10... | collective-permute-start | bytes 1572872 | tf_op jit(solution)/shard_map/ppermute | solution.py:30
  318.7 3.5 reshape.66.refs_1_
  322.3 3.5 reshape.68.refs_2_
  325.8 3.6 reshape.70.refs_3_
  329.5 10.7 %collective-permute-start.13 = (bf16[256,1024]{1,0:T(8,128)(2,1)}, bf16[256,1024]{1,0:T(8,128)(2,1)S(1)}, u32[]{:S(2)}, u32[]{:S(2)}) collective-permute-start(bf16[256,1024]{1,0:T(8,128)(2,1)} %slice.52), channel_id=1, source_target_pairs={{0,8},{8,16},{16,24},{24,0},{1,9},{9,17},{17,25},{25,1},{2,10},{10... | collective-permute-start | bytes 1572872 | tf_op jit(solution)/shard_map/ppermute | solution.py:30
  341.4 13.0 %shard_map.59.refs_9_ = bf16[2048,3584]{1,0:T(8,128)(2,1)} custom-call(bf16[504,2048]{1,0:T(8,128)(2,1)S(1)} %reshape.64.refs_0_, bf16[504,2048]{1,0:T(8,128)(2,1)} %reshape.66.refs_1_, bf16[504,2048]{1,0:T(8,128)(2,1)} %reshape.68.refs_2_, bf16[504,2048]{1,0:T(8,128)(2,1)} %reshape.70.refs_3_, bf16[504,1024]{1,0:T(8,128)(2,1)} %get-tuple-element.2.refs_4_, ...), custom_call_target="tpu_custom_call" | custom-call | flops 8455716864 | bytes 16580608 | tf_op jit(solution)/shard_map/pallas_call | solution.py:83
  354.9 12.2 %shard_map.60.refs_9_ = bf16[2048,3584]{1,0:T(8,128)(2,1)} custom-call(bf16[504,2048]{1,0:T(8,128)(2,1)S(1)} %reshape.64.refs_0_, bf16[504,2048]{1,0:T(8,128)(2,1)} %reshape.66.refs_1_, bf16[504,2048]{1,0:T(8,128)(2,1)} %reshape.68.refs_2_, bf16[504,2048]{1,0:T(8,128)(2,1)} %reshape.70.refs_3_, ...), custom_call_target="tpu_custom_call", output_to_operand_aliasing={{}: (9, {})} | custom-call | flops 8455716864 | bytes 16580608 | tf_op jit(solution)/shard_map/pallas_call | solution.py:83
  367.1 10.6 %collective-permute-done.14.refs_8_ = bf16[248,1024]{1,0:T(8,128)(2,1)S(1)} collective-permute-done((bf16[248,1024]{1,0:T(8,128)(2,1)S(1)}, bf16[248,1024]{1,0:T(8,128)(2,1)S(1)}, u32[]{:S(2)}, u32[]{:S(2)}) %collective-permute-start.14) | collective-permute-done | bytes 507936 | tf_op jit(solution)/shard_map/ppermute | solution.py:30
  377.6 12.0 %shard_map.61.refs_9_ = bf16[2048,3584]{1,0:T(8,128)(2,1)} custom-call(bf16[504,2048]{1,0:T(8,128)(2,1)S(1)} %reshape.64.refs_0_, bf16[504,2048]{1,0:T(8,128)(2,1)} %reshape.66.refs_1_, bf16[504,2048]{1,0:T(8,128)(2,1)} %reshape.68.refs_2_, bf16[504,2048]{1,0:T(8,128)(2,1)} %reshape.70.refs_3_, ...), custom_call_target="tpu_custom_call", output_to_operand_aliasing={{}: (9, {})} | custom-call | flops 8455716864 | bytes 16580608 | tf_op jit(solution)/shard_map/pallas_call | solution.py:83
  389.6 8.0 %shard_map.62 = bf16[2048,3584]{1,0:T(8,128)(2,1)} custom-call(bf16[504,2048]{1,0:T(8,128)(2,1)S(1)} %reshape.64.refs_0_, bf16[504,2048]{1,0:T(8,128)(2,1)S(1)} %copy-done, bf16[504,2048]{1,0:T(8,128)(2,1)} %reshape.68.refs_2_, bf16[504,2048]{1,0:T(8,128)(2,1)} %reshape.70.refs_3_, bf16[504,512]{1,0:T(8,128)(2,1)} %slice.48.refs_4_, ...), custom_call_target="tpu_custom_call", output_to_operand_aliasing={{}: (9, {})} | custom-call | flops 4227858432 | bytes 12419072 | tf_op jit(solution)/shard_map/pallas_call | solution.py:83
  (118 shorter events, 64.8 us)
Async XLA Ops:
  5.0 55.9 %all-to-all-start.1 = ((bf16[8,63,2048]{2,1,0:T(8,128)(2,1)}), bf16[8,63,2048]{2,1,0:T(8,128)(2,1)S(1)}, u32[]{:S(2)}, u32[]{:S(2)}) async-start(bf16[8,63,2048]{2,1,0:T(8,128)(2,1)} %bitcast.43), calls=%async_computation.1 | async-start | bytes 4194304 | tf_op jit(solution)/shard_map/all_to_all | solution.py:139
  29.8 28.2 %collective-permute-start = (bf16[4,63,2048]{2,0,1:T(4,128)(2,1)}, bf16[4,63,2048]{2,0,1:T(4,128)(2,1)S(1)}, u32[]{:S(2)}, u32[]{:S(2)}) collective-permute-start(bf16[4,63,2048]{2,0,1:T(4,128)(2,1)} %copy.33), channel_id=1, source_target_pairs={{0,1},{1,0},{2,3},{3,2},{4,5},{5,4},{6,7},{7,6},{8,9},{9,8},{10,11... | collective-permute-start | bytes 3096584 | tf_op jit(solution)/shard_map/ppermute | solution.py:30
  60.9 22.4 %all-to-all-start = ((bf16[4,63,2048]{2,1,0:T(8,128)(2,1)}), bf16[4,63,2048]{2,1,0:T(8,128)(2,1)}, u32[]{:S(2)}, u32[]{:S(2)}) async-start(bf16[4,63,2048]{2,1,0:T(8,128)(2,1)} %fusion.6), calls=%async_computation | async-start | bytes 2097152 | tf_op jit(solution)/shard_map/all_to_all | solution.py:127
  65.3 15.0 %collective-permute-start.2 = (bf16[112,2048]{1,0:T(8,128)(2,1)S(1)}, bf16[112,2048]{1,0:T(8,128)(2,1)S(1)}, u32[]{:S(2)}, u32[]{:S(2)}) collective-permute-start(bf16[112,2048]{1,0:T(8,128)(2,1)S(1)} %copy-done.16), channel_id=1, source_target_pairs={{0,8},{8,16},{16,24},{24,0},{1,9},{9,17},{17,25},{25,1},{2,10},{10... | collective-permute-start | bytes 1376264 | tf_op jit(solution)/shard_map/ppermute | solution.py:30
  66.9 13.2 %collective-permute-start.1 = (s32[2,112]{1,0:T(2,128)S(1)}, s32[2,112]{1,0:T(2,128)S(1)}, u32[]{:S(2)}, u32[]{:S(2)}) collective-permute-start(s32[2,112]{1,0:T(2,128)S(1)} %bitcast.48), channel_id=1, source_target_pairs={{0,8},{8,16},{16,24},{24,0},{1,9},{9,17},{17,25},{25,1},{2,10},{10... | collective-permute-start | bytes 2696 | tf_op jit(solution)/shard_map/ppermute | solution.py:30
  84.9 29.4 %all-to-all-start.2 = ((bf16[8,63,2048]{2,1,0:T(8,128)(2,1)}), bf16[8,63,2048]{2,1,0:T(8,128)(2,1)S(1)}, u32[]{:S(2)}, u32[]{:S(2)}) async-start(bf16[8,63,2048]{2,1,0:T(8,128)(2,1)} %bitcast.45), calls=%async_computation.2 | async-start | bytes 4194304 | tf_op jit(solution)/shard_map/all_to_all | solution.py:139
  88.7 13.1 %collective-permute-start.4 = (bf16[112,2048]{1,0:T(8,128)(2,1)S(1)}, bf16[112,2048]{1,0:T(8,128)(2,1)S(1)}, u32[]{:S(2)}, u32[]{:S(2)}) collective-permute-start(bf16[112,2048]{1,0:T(8,128)(2,1)S(1)} %copy-done.17), channel_id=1, source_target_pairs={{0,24},{8,0},{16,8},{24,16},{1,25},{9,1},{17,9},{25,17},{2,26},{10... | collective-permute-start | bytes 1376264 | tf_op jit(solution)/shard_map/ppermute | solution.py:30
  90.5 11.1 %collective-permute-start.3 = (s32[2,112]{1,0:T(2,128)S(1)}, s32[2,112]{1,0:T(2,128)S(1)}, u32[]{:S(2)}, u32[]{:S(2)}) collective-permute-start(s32[2,112]{1,0:T(2,128)S(1)} %bitcast.49), channel_id=1, source_target_pairs={{0,24},{8,0},{16,8},{24,16},{1,25},{9,1},{17,9},{25,17},{2,26},{10... | collective-permute-start | bytes 2696 | tf_op jit(solution)/shard_map/ppermute | solution.py:30
  116.4 43.3 %all-to-all-start.3 = ((bf16[8,63,2048]{2,1,0:T(8,128)(2,1)}), bf16[8,63,2048]{2,1,0:T(8,128)(2,1)}, u32[]{:S(2)}, u32[]{:S(2)}) async-start(bf16[8,63,2048]{2,1,0:T(8,128)(2,1)} %bitcast.44), calls=%async_computation.3 | async-start | bytes 4194304 | tf_op jit(solution)/shard_map/all_to_all | solution.py:139
  120.7 11.8 %collective-permute-start.5 = (s32[2,112]{1,0:T(2,128)S(1)}, s32[2,112]{1,0:T(2,128)S(1)}, u32[]{:S(2)}, u32[]{:S(2)}) collective-permute-start(s32[2,112]{1,0:T(2,128)S(1)} %bitcast.50), channel_id=1, source_target_pairs={{0,16},{8,24},{16,0},{24,8},{1,17},{9,25},{17,1},{25,9},{2,18},{10... | collective-permute-start | bytes 2696 | tf_op jit(solution)/shard_map/ppermute | solution.py:30
  121.5 35.2 %collective-permute-start.6 = (bf16[112,2048]{1,0:T(8,128)(2,1)S(1)}, bf16[112,2048]{1,0:T(8,128)(2,1)S(1)}, u32[]{:S(2)}, u32[]{:S(2)}) collective-permute-start(bf16[112,2048]{1,0:T(8,128)(2,1)S(1)} %copy-done.18), channel_id=1, source_target_pairs={{0,16},{8,24},{16,0},{24,8},{1,17},{9,25},{17,1},{25,9},{2,18},{10... | collective-permute-start | bytes 1376264 | tf_op jit(solution)/shard_map/ppermute | solution.py:30
  125.6 42.2 %collective-permute-start.7 = (bf16[504,512]{1,0:T(8,128)(2,1)}, bf16[504,512]{1,0:T(8,128)(2,1)}, u32[]{:S(2)}, u32[]{:S(2)}) collective-permute-start(bf16[504,512]{1,0:T(8,128)(2,1)} %slice.48.refs_4_), channel_id=1, source_target_pairs={{0,8},{8,16},{16,24},{24,0},{1,9},{9,17},{17,25},{25,1},{2,10},{10... | collective-permute-start | bytes 1548296 | tf_op jit(solution)/shard_map/ppermute | solution.py:30
  125.6 56.4 %collective-permute-start.8 = (bf16[504,512]{1,0:T(8,128)(2,1)}, bf16[504,512]{1,0:T(8,128)(2,1)}, u32[]{:S(2)}, u32[]{:S(2)}) collective-permute-start(bf16[504,512]{1,0:T(8,128)(2,1)} %slice.48.refs_4_), channel_id=1, source_target_pairs={{0,24},{8,0},{16,8},{24,16},{1,25},{9,1},{17,9},{25,17},{2,26},{10... | collective-permute-start | bytes 1548296 | tf_op jit(solution)/shard_map/ppermute | solution.py:30
  132.5 35.3 %copy-start.1 = (bf16[504,1024]{1,0:T(8,128)(2,1)}, bf16[504,1024]{1,0:T(8,128)(2,1)S(1)}, u32[]{:S(2)}) copy-start(bf16[504,1024]{1,0:T(8,128)(2,1)S(1)} %get-tuple-element.3.refs_4_) | copy-start | bytes 3096580
  132.5 58.0 %collective-permute-start.19 = (bf16[504,1024]{1,0:T(8,128)(2,1)}, bf16[504,1024]{1,0:T(8,128)(2,1)}, u32[]{:S(2)}, u32[]{:S(2)}) collective-permute-start(bf16[504,1024]{1,0:T(8,128)(2,1)} %get-tuple-element.2.refs_4_), channel_id=1, source_target_pairs={{0,8},{8,16},{16,24},{24,0},{1,9},{9,17},{17,25},{25,1},{2,10},{10... | collective-permute-start | bytes 3096584 | tf_op jit(solution)/shard_map/ppermute | solution.py:30
  161.4 164.4 %all-to-all-start.4 = ((bf16[8,63,2048]{2,1,0:T(8,128)(2,1)}), bf16[8,63,2048]{2,1,0:T(8,128)(2,1)}, u32[]{:S(2)}, u32[]{:S(2)}) async-start(bf16[8,63,2048]{2,1,0:T(8,128)(2,1)} %bitcast.42), calls=%async_computation.4 | async-start | bytes 4194304 | tf_op jit(solution)/shard_map/all_to_all | solution.py:139
  165.7 60.4 %collective-permute-start.20 = (bf16[504,1024]{1,0:T(8,128)(2,1)}, bf16[504,1024]{1,0:T(8,128)(2,1)S(1)}, u32[]{:S(2)}, u32[]{:S(2)}) collective-permute-start(bf16[504,1024]{1,0:T(8,128)(2,1)} %get-tuple-element.2.refs_4_), channel_id=1, source_target_pairs={{0,24},{8,0},{16,8},{24,16},{1,25},{9,1},{17,9},{25,17},{2,26},{10... | collective-permute-start | bytes 3096584 | tf_op jit(solution)/shard_map/ppermute | solution.py:30
  165.8 69.8 %collective-permute-start.15 = (bf16[504,1024]{1,0:T(8,128)(2,1)S(1)}, bf16[504,1024]{1,0:T(8,128)(2,1)S(1)}, u32[]{:S(2)}, u32[]{:S(2)}) collective-permute-start(bf16[504,1024]{1,0:T(8,128)(2,1)S(1)} %get-tuple-element.3.refs_4_), channel_id=1, source_target_pairs={{0,8},{8,16},{16,24},{24,0},{1,9},{9,17},{17,25},{25,1},{2,10},{10... | collective-permute-start | bytes 3096584 | tf_op jit(solution)/shard_map/ppermute | solution.py:30
  167.8 102.6 %collective-permute-start.16 = (bf16[504,1024]{1,0:T(8,128)(2,1)S(1)}, bf16[504,1024]{1,0:T(8,128)(2,1)S(1)}, u32[]{:S(2)}, u32[]{:S(2)}) collective-permute-start(bf16[504,1024]{1,0:T(8,128)(2,1)S(1)} %get-tuple-element.3.refs_4_), channel_id=1, source_target_pairs={{0,24},{8,0},{16,8},{24,16},{1,25},{9,1},{17,9},{25,17},{2,26},{10... | collective-permute-start | bytes 3096584 | tf_op jit(solution)/shard_map/ppermute | solution.py:30
  182.0 97.8 %collective-permute-start.11 = (bf16[504,1024]{1,0:T(8,128)(2,1)S(1)}, bf16[504,1024]{1,0:T(8,128)(2,1)S(1)}, u32[]{:S(2)}, u32[]{:S(2)}) collective-permute-start(bf16[504,1024]{1,0:T(8,128)(2,1)S(1)} %get-tuple-element.4.refs_4_), channel_id=1, source_target_pairs={{0,8},{8,16},{16,24},{24,0},{1,9},{9,17},{17,25},{25,1},{2,10},{10... | collective-permute-start | bytes 3096584 | tf_op jit(solution)/shard_map/ppermute | solution.py:30
  190.6 113.2 %collective-permute-start.12 = (bf16[504,1024]{1,0:T(8,128)(2,1)S(1)}, bf16[504,1024]{1,0:T(8,128)(2,1)S(1)}, u32[]{:S(2)}, u32[]{:S(2)}) collective-permute-start(bf16[504,1024]{1,0:T(8,128)(2,1)S(1)} %get-tuple-element.4.refs_4_), channel_id=1, source_target_pairs={{0,24},{8,0},{16,8},{24,16},{1,25},{9,1},{17,9},{25,17},{2,26},{10... | collective-permute-start | bytes 3096584 | tf_op jit(solution)/shard_map/ppermute | solution.py:30
  226.1 68.6 %copy-start.11 = (bf16[504,1024]{1,0:T(8,128)(2,1)}, bf16[504,1024]{1,0:T(8,128)(2,1)S(1)}, u32[]{:S(2)}) copy-start(bf16[504,1024]{1,0:T(8,128)(2,1)S(1)} %collective-permute-done.20.refs_6_) | copy-start | bytes 3096580
  226.1 103.3 %collective-permute-start.21 = (bf16[256,1024]{1,0:T(8,128)(2,1)}, bf16[256,1024]{1,0:T(8,128)(2,1)}, u32[]{:S(2)}, u32[]{:S(2)}) collective-permute-start(bf16[256,1024]{1,0:T(8,128)(2,1)} %slice.58), channel_id=1, source_target_pairs={{0,8},{8,16},{16,24},{24,0},{1,9},{9,17},{17,25},{25,1},{2,10},{10... | collective-permute-start | bytes 1572872 | tf_op jit(solution)/shard_map/ppermute | solution.py:30
  235.5 76.8 %copy-start.3 = (bf16[504,1024]{1,0:T(8,128)(2,1)}, bf16[504,1024]{1,0:T(8,128)(2,1)S(1)}, u32[]{:S(2)}) copy-start(bf16[504,1024]{1,0:T(8,128)(2,1)S(1)} %collective-permute-done.15.refs_5_) | copy-start | bytes 3096580
  235.5 93.8 %collective-permute-start.22 = (bf16[248,1024]{1,0:T(8,128)(2,1)}, bf16[248,1024]{1,0:T(8,128)(2,1)}, u32[]{:S(2)}, u32[]{:S(2)}) collective-permute-start(bf16[248,1024]{1,0:T(8,128)(2,1)} %slice.59), channel_id=1, source_target_pairs={{0,24},{8,0},{16,8},{24,16},{1,25},{9,1},{17,9},{25,17},{2,26},{10... | collective-permute-start | bytes 1523720 | tf_op jit(solution)/shard_map/ppermute | solution.py:30
  270.4 41.9 %copy-start.7 = (bf16[504,1024]{1,0:T(8,128)(2,1)}, bf16[504,1024]{1,0:T(8,128)(2,1)S(1)}, u32[]{:S(2)}) copy-start(bf16[504,1024]{1,0:T(8,128)(2,1)S(1)} %collective-permute-done.16.refs_6_) | copy-start | bytes 3096580
  270.4 119.2 %collective-permute-start.9 = (bf16[256,512]{1,0:T(8,128)(2,1)}, bf16[256,512]{1,0:T(8,128)(2,1)S(1)}, u32[]{:S(2)}, u32[]{:S(2)}) collective-permute-start(bf16[256,512]{1,0:T(8,128)(2,1)} %slice.49), channel_id=1, source_target_pairs={{0,8},{8,16},{16,24},{24,0},{1,9},{9,17},{17,25},{25,1},{2,10},{10... | collective-permute-start | bytes 786440 | tf_op jit(solution)/shard_map/ppermute | solution.py:30
  279.8 109.8 %collective-permute-start.10 = (bf16[248,512]{1,0:T(8,128)(2,1)}, bf16[248,512]{1,0:T(8,128)(2,1)}, u32[]{:S(2)}, u32[]{:S(2)}) collective-permute-start(bf16[248,512]{1,0:T(8,128)(2,1)} %slice.50), channel_id=1, source_target_pairs={{0,24},{8,0},{16,8},{24,16},{1,25},{9,1},{17,9},{25,17},{2,26},{10... | collective-permute-start | bytes 761864 | tf_op jit(solution)/shard_map/ppermute | solution.py:30
  303.7 51.1 %collective-permute-start.17 = (bf16[256,1024]{1,0:T(8,128)(2,1)}, bf16[256,1024]{1,0:T(8,128)(2,1)}, u32[]{:S(2)}, u32[]{:S(2)}) collective-permute-start(bf16[256,1024]{1,0:T(8,128)(2,1)} %slice.55), channel_id=1, source_target_pairs={{0,8},{8,16},{16,24},{24,0},{1,9},{9,17},{17,25},{25,1},{2,10},{10... | collective-permute-start | bytes 1572872 | tf_op jit(solution)/shard_map/ppermute | solution.py:30
  329.4 25.0 %collective-permute-start.18 = (bf16[248,1024]{1,0:T(8,128)(2,1)}, bf16[248,1024]{1,0:T(8,128)(2,1)S(1)}, u32[]{:S(2)}, u32[]{:S(2)}) collective-permute-start(bf16[248,1024]{1,0:T(8,128)(2,1)} %slice.56), channel_id=1, source_target_pairs={{0,24},{8,0},{16,8},{24,16},{1,25},{9,1},{17,9},{25,17},{2,26},{10... | collective-permute-start | bytes 1523720 | tf_op jit(solution)/shard_map/ppermute | solution.py:30
  329.5 48.2 %collective-permute-start.13 = (bf16[256,1024]{1,0:T(8,128)(2,1)}, bf16[256,1024]{1,0:T(8,128)(2,1)S(1)}, u32[]{:S(2)}, u32[]{:S(2)}) collective-permute-start(bf16[256,1024]{1,0:T(8,128)(2,1)} %slice.52), channel_id=1, source_target_pairs={{0,8},{8,16},{16,24},{24,0},{1,9},{9,17},{17,25},{25,1},{2,10},{10... | collective-permute-start | bytes 1572872 | tf_op jit(solution)/shard_map/ppermute | solution.py:30
  354.4 23.3 %collective-permute-start.14 = (bf16[248,1024]{1,0:T(8,128)(2,1)S(1)}, bf16[248,1024]{1,0:T(8,128)(2,1)S(1)}, u32[]{:S(2)}, u32[]{:S(2)}) collective-permute-start(bf16[248,1024]{1,0:T(8,128)(2,1)S(1)} %copy-done.15), channel_id=1, source_target_pairs={{0,24},{8,0},{16,8},{24,16},{1,25},{9,1},{17,9},{25,17},{2,26},{10... | collective-permute-start | bytes 1523720 | tf_op jit(solution)/shard_map/ppermute | solution.py:30
  (16 other events, 266.4 us)
